TPU v7x, 32 devices: a whole 2x2x4 slice. The times are simulated.
32 devices in a mesh: up: 8 (over y, x, core), dn: 4 (over z).
Axes of the slice: x: 2, y: 2, z: 4, core: 2. Of those that a mesh axis runs over, the one named last changes fastest.
Arguments:
- start_vector: bfloat16 [13312, 13312], P('up', 'dn'), may hold values from -6 to 6
- hop_tiles: bfloat16 [104, 5, 128, 128], replicated, may hold values from -0.5 to 0.5
- tile_columns: int32 [104, 5], replicated, may hold values from 0 to 103, as said below
- tile_signs: int32 [104, 5], replicated, may hold values from 0 to 1
- occupation: int32 [16, 13312], replicated, may hold values from 0 to 1, as said below
Outputs:
- next_vector: bfloat16 [13312, 13312], P('up', 'dn')
- alphas: float32 [2], replicated
- betas: float32 [2], replicated
Inputs may be any that keep to these rules, and one draw needn't show every extreme that they name: Each row of tile_columns names 5 different tile columns. Every column of occupation holds exactly 8 ones.
All inputs are finite; a program needn't handle non-finite values.
Results may differ from a plain program's by a relative error of at most 0.0065.
Values may be sent and summed in bfloat16 or wider, within the bound.
A program may use at most 256 MiB of HBM per device.

v0:
```python
import jax
import jax.numpy as jnp
from jax import lax
from jax.sharding import PartitionSpec as P

STEPS = 2
coupling = 4.0


def hop_lead(matrix, signed, tile_columns):
    layout = matrix.shape
    tile_width = signed.shape[-1]
    cube = matrix.reshape(layout[0] // tile_width, tile_width, -1)
    picked = cube[tile_columns]
    result = jnp.einsum("ikab,ikbm->iam", signed, picked, preferred_element_type=jnp.float32)
    return result.reshape(layout).astype(jnp.bfloat16)


def body(start_vector, hop_tiles, tile_columns, tile_signs, occupation):
    signed = hop_tiles * (1 - 2 * tile_signs).astype(jnp.bfloat16)[:, :, None, None]
    rows_local, cols_local = start_vector.shape
    count_up = lax.axis_size("up")
    count_down = lax.axis_size("dn")
    row_start = lax.axis_index("up") * rows_local
    col_start = lax.axis_index("dn") * cols_local
    block_rows, block_cols = start_vector.shape
    occ_rows = lax.dynamic_slice_in_dim(occupation, row_start, block_rows, 1).astype(jnp.bfloat16)
    occ_cols = lax.dynamic_slice_in_dim(occupation, col_start, block_cols, 1).astype(jnp.bfloat16)
    diagonal = coupling * jnp.einsum(
        "sa,sb->ab", occ_rows, occ_cols, preferred_element_type=jnp.float32
    )
    vector = start_vector.astype(jnp.float32)
    total = lax.psum(jnp.sum(vector * vector), ("up", "dn"))
    vector = vector / jnp.maximum(jnp.sqrt(total), 1.0)
    length = total / jnp.maximum(total, 1.0)
    previous = jnp.zeros_like(vector)
    beta_value = jnp.float32(0.0)
    alpha_list = []
    beta_list = []
    for iteration in range(STEPS):
        rounded = vector.astype(jnp.bfloat16)
        cube = rounded.reshape(block_rows, count_up, block_cols // count_up)
        up_part = lax.all_to_all(cube, "up", split_axis=1, concat_axis=0, tiled=True)
        up_whole = up_part.reshape(up_part.shape[0], up_part.shape[2])
        up_hopped = hop_lead(up_whole, signed, tile_columns).reshape(up_part.shape)
        moved = lax.all_to_all(up_hopped, "up", split_axis=0, concat_axis=1, tiled=True)
        hopped_up = moved.reshape(block_rows, block_cols)
        flipped = rounded.T.reshape(block_cols, count_down, block_rows // count_down)
        part = lax.all_to_all(flipped, "dn", split_axis=1, concat_axis=0, tiled=True)
        whole = part.reshape(part.shape[0], part.shape[2])
        hopped = hop_lead(whole, signed, tile_columns).reshape(part.shape)
        returned = lax.all_to_all(hopped, "dn", split_axis=0, concat_axis=1, tiled=True)
        hopped_down = returned.reshape(block_cols, block_rows).T
        work = (
            hopped_up.astype(jnp.float32)
            + hopped_down.astype(jnp.float32)
            + diagonal * vector
            - beta_value * previous
        )
        intersect, square = lax.psum((jnp.sum(work * vector), jnp.sum(work * work)), ("up", "dn"))
        work = work - intersect * vector
        residual = square - 2.0 * intersect * intersect + intersect * intersect * length
        beta_value = jnp.sqrt(jnp.maximum(residual, 1.0))
        length = residual / jnp.maximum(residual, 1.0)
        previous = vector
        vector = work / beta_value
        alpha_list.append(intersect)
        beta_list.append(beta_value)
    final = vector.astype(jnp.bfloat16)
    return (final, jnp.stack(alpha_list), jnp.stack(beta_list))


def solution(mesh):
    placed = (P("up", "dn"), P(), P(), P(), P())
    return jax.shard_map(
        body, mesh=mesh, in_specs=placed, out_specs=(P("up", "dn"), P(), P()), check_vma=False
    )
```

profile of v0, /device:TPU:12, one launch (start us, length us, event | category | flops | bytes accessed | tf_op | source)
XLA Modules:
  0.0 2605.0 jit_solution(15196336587195113989)
XLA Ops:
  11.1 41.6 %psum.35 = f32[]{:T(128)} all-reduce(f32[]{:T(128)} %fusion), channel_id=1, replica_groups=mesh['up'=8,'dn'=4] {'up','dn'}, use_global_device_ids=true, to_apply=%region_1.0 | all-reduce | flops 1 | bytes 8 | tf_op jit(solution)/shard_map/psum | solution.py:33
  53.3 10.6 fusion.26
  64.0 16.3 copy.62
  80.3 127.1 %all_to_all.96 = bf16[1664,8,416]{0,2,1:T(8,128)(2,1)} all-to-all(bf16[1664,8,416]{0,2,1:T(8,128)(2,1)} %bitcast.112), channel_id=1, replica_groups=mesh['up'=8,'dn'=4] {'up'}, dimensions={1} | all-to-all | bytes 22151168 | tf_op jit(solution)/shard_map/all_to_all | solution.py:43
  214.7 18.8 copy.63
  233.4 21.0 reshape_reshape.12
  254.5 10.7 copy.65
  265.2 26.4 %gather_fusion = bf16[520,128,416]{1,2,0:T(8,128)(2,1)} fusion(bf16[104,128,416]{1,2,0:T(8,128)(2,1)} %copy.65, s32[1024]{0:T(1024)S(1)} %pad_clamp_fusion), kind=kCustom, calls=%fused_computation | custom fusion | bytes 110757920 | tf_op jit(solution)/shard_map/gather | solution.py:14
  291.6 29.5 %bitcast_convert_fusion.3 = bf16[104,128,416]{1,2,0:T(8,128)(2,1)} fusion(bf16[104,5,128,416]{2,3,1,0:T(8,128)(2,1)} %bitcast.107, bf16[104,5,128,128]{3,2,1,0:T(8,128)(2,1)} %param.6, bf16[104,5]{1,0:T(8,128)(2,1)S(1)} %copy.61), kind=kOutput, calls=%fused_computation.15 | convolution fusion | flops 7102431232 | bytes 83493904 | tf_op jit(solution)/shard_map/ikab,ikbm->iam/dot_general | solution.py:15
  321.1 16.3 copy.95
  337.4 77.7 %reshape.155 = bf16[13312,1,416]{2,1,0:T(2,128)(2,1)} reshape(bf16[104,128,416]{2,1,0:T(8,128)(2,1)} %copy.95) | data formatting | bytes 22151168 | tf_op jit(solution)/shard_map/convert_element_type | solution.py:16
  415.7 87.5 %reduce = bf16[13312,416]{1,0:T(8,128)(2,1)} reduce(bf16[13312,1,416]{2,1,0:T(2,128)(2,1)} %reshape.155, bf16[]{:T(256)} %broadcast.21), dimensions={1}, to_apply=%reshape.155.reduce_sub_computation | reduce | bytes 22151170 | tf_op jit(solution)/shard_map/convert_element_type | solution.py:16
  503.1 21.7 reshape.159
  531.9 26.0 copy.70
  557.9 18.8 reshape_reshape.13
  587.4 26.4 %gather_fusion.1 = bf16[520,128,416]{1,2,0:T(8,128)(2,1)} fusion(bf16[104,128,416]{1,2,0:T(8,128)(2,1)} %copy.71, s32[1024]{0:T(1024)S(1)} %pad_clamp_fusion), kind=kCustom, calls=%fused_computation.1 | custom fusion | bytes 110757920 | tf_op jit(solution)/shard_map/gather | solution.py:14
  613.8 29.4 %bitcast_convert_fusion.2 = bf16[104,128,416]{1,2,0:T(8,128)(2,1)} fusion(bf16[104,5,128,416]{2,3,1,0:T(8,128)(2,1)} %bitcast.108, bf16[104,5,128,128]{3,2,1,0:T(8,128)(2,1)} %param.6, bf16[104,5]{1,0:T(8,128)(2,1)S(1)} %copy.61), kind=kOutput, calls=%fused_computation.14 | convolution fusion | flops 7102431232 | bytes 83493904 | tf_op jit(solution)/shard_map/ikab,ikbm->iam/dot_general | solution.py:15
  643.2 16.3 copy.96
  659.6 77.6 %reshape.156 = bf16[13312,1,416]{2,1,0:T(2,128)(2,1)} reshape(bf16[104,128,416]{2,1,0:T(8,128)(2,1)} %copy.96) | data formatting | bytes 22151168 | tf_op jit(solution)/shard_map/convert_element_type | solution.py:16
  737.1 87.6 %reduce.1 = bf16[13312,416]{1,0:T(8,128)(2,1)} reduce(bf16[13312,1,416]{2,1,0:T(2,128)(2,1)} %reshape.156, bf16[]{:T(256)} %broadcast.21), dimensions={1}, to_apply=%reshape.156.reduce_sub_computation | reduce | bytes 22151170 | tf_op jit(solution)/shard_map/convert_element_type | solution.py:16
  824.8 22.4 reshape.161
  854.8 30.4 %reshape.160 = bf16[13312,1,416]{2,1,0:T(2,128)(2,1)} reshape(bf16[8,2,346112]{2,1,0:T(2,128)(2,1)} %all-to-all-done.1) | data formatting | bytes 22151168
  885.3 52.5 %copy.68 = bf16[13312,1,416]{0,2,1:T(8,128)(2,1)} copy(bf16[13312,1,416]{2,1,0:T(2,128)(2,1)} %reshape.160) | data formatting | bytes 22151168 | tf_op jit(solution)/shard_map/all_to_all | solution.py:46
  953.0 19.4 copy.69
  972.4 22.9 copy.76
  995.2 96.4 %all-to-all-done.3 = bf16[4,2,692224]{2,1,0:T(2,128)(2,1)} async-done(((bf16[4,2,692224]{2,1,0:T(2,128)(2,1)}), bf16[4,2,692224]{2,1,0:T(2,128)(2,1)}, u32[]{:S(2)}, u32[]{:S(2)}) %all-to-all-start.3) | async-done | bytes 11075616 | tf_op jit(solution)/shard_map/all_to_all | solution.py:52
  1091.6 45.3 %reshape.162 = bf16[13312,1,416]{2,1,0:T(2,128)(2,1)} reshape(bf16[4,2,692224]{2,1,0:T(2,128)(2,1)} %all-to-all-done.3) | data formatting | bytes 22151168
  1136.9 52.8 %copy.74 = bf16[13312,1,416]{0,2,1:T(8,128)(2,1)} copy(bf16[13312,1,416]{2,1,0:T(2,128)(2,1)} %reshape.162) | data formatting | bytes 22151168 | tf_op jit(solution)/shard_map/all_to_all | solution.py:52
  1189.8 21.5 reshape.109
  1211.3 19.4 copy.75
  1230.7 32.3 %multiply_reduce_fusion.3 = (f32[]{:T(128)}, f32[]{:T(128)}, f32[1664,3328]{1,0:T(8,128)}, f32[1664,3328]{1,0:T(8,128)}) fusion(f32[]{:T(128)S(6)} %max.13, bf16[1664,3328]{1,0:T(8,128)(2,1)} %param.5, f32[1664,3328]{1,0:T(8,128)} %copy.76, f32[3328,4,1,416]{0,3,1,2:T(8,128)} %copy.75, s32[16,13312]{1,0:T(8,128)} %param.9, s32[]{:T(128)S(6)} %select_n.14, ...), kind=kOutput, calls=%fused_computation.21 | convolution fusion | flops 232667136 | bytes 99999760 | tf_op jit(solution)/shard_map/sa,sb->ab/dot_general | solution.py:29
  1263.1 43.3 %all-reduce.1 = (f32[]{:T(128)}, f32[]{:T(128)}) all-reduce(f32[]{:T(128)} %get-tuple-element.6, f32[]{:T(128)} %get-tuple-element.5), channel_id=1, replica_groups=mesh['up'=8,'dn'=4] {'up','dn'}, use_global_device_ids=true, to_apply=%region_5.0 | all-reduce | flops 2 | bytes 16 | tf_op jit(solution)/shard_map/psum | solution.py:60
  1309.6 22.7 fusion.28
  1332.2 16.3 copy.77
  1348.6 127.0 %all_to_all.97 = bf16[1664,8,416]{0,2,1:T(8,128)(2,1)} all-to-all(bf16[1664,8,416]{0,2,1:T(8,128)(2,1)} %bitcast.113), channel_id=1, replica_groups=mesh['up'=8,'dn'=4] {'up'}, dimensions={1} | all-to-all | bytes 22151168 | tf_op jit(solution)/shard_map/all_to_all | solution.py:43
  1481.8 18.8 copy.78
  1500.6 21.0 reshape_reshape.14
  1521.6 10.7 copy.79
  1532.3 26.5 %gather_fusion.2 = bf16[520,128,416]{1,2,0:T(8,128)(2,1)} fusion(bf16[104,128,416]{1,2,0:T(8,128)(2,1)} %copy.79, s32[1024]{0:T(1024)S(1)} %copy-done.1), kind=kCustom, calls=%fused_computation.2 | custom fusion | bytes 110757920 | tf_op jit(solution)/shard_map/gather | solution.py:14
  1558.8 29.4 %bitcast_convert_fusion.1 = bf16[104,128,416]{1,2,0:T(8,128)(2,1)} fusion(bf16[104,5,128,416]{2,3,1,0:T(8,128)(2,1)} %bitcast.109, bf16[104,5,128,128]{3,2,1,0:T(8,128)(2,1)} %param.6, bf16[104,5]{1,0:T(8,128)(2,1)S(1)} %copy-done.3), kind=kOutput, calls=%fused_computation.13 | convolution fusion | flops 7102431232 | bytes 83493904 | tf_op jit(solution)/shard_map/ikab,ikbm->iam/dot_general | solution.py:15
  1588.2 16.3 copy.97
  1604.5 77.7 %reshape.157 = bf16[13312,1,416]{2,1,0:T(2,128)(2,1)} reshape(bf16[104,128,416]{2,1,0:T(8,128)(2,1)} %copy.97) | data formatting | bytes 22151168 | tf_op jit(solution)/shard_map/convert_element_type | solution.py:16
  1682.3 87.5 %reduce.2 = bf16[13312,416]{1,0:T(8,128)(2,1)} reduce(bf16[13312,1,416]{2,1,0:T(2,128)(2,1)} %reshape.157, bf16[]{:T(256)} %broadcast.21), dimensions={1}, to_apply=%reshape.157.reduce_sub_computation | reduce | bytes 22151170 | tf_op jit(solution)/shard_map/convert_element_type | solution.py:16
  1769.7 21.7 reshape.163
  1798.5 26.0 copy.84
  1824.5 18.8 reshape_reshape.15
  1854.0 26.4 %gather_fusion.3 = bf16[520,128,416]{1,2,0:T(8,128)(2,1)} fusion(bf16[104,128,416]{1,2,0:T(8,128)(2,1)} %copy.85, s32[1024]{0:T(1024)S(1)} %copy-done.1), kind=kCustom, calls=%fused_computation.3 | custom fusion | bytes 110757920 | tf_op jit(solution)/shard_map/gather | solution.py:14
  1880.4 29.4 %bitcast_convert_fusion = bf16[104,128,416]{1,2,0:T(8,128)(2,1)} fusion(bf16[104,5,128,416]{2,3,1,0:T(8,128)(2,1)} %bitcast.106, bf16[104,5,128,128]{3,2,1,0:T(8,128)(2,1)} %param.6, bf16[104,5]{1,0:T(8,128)(2,1)S(1)} %copy-done.3), kind=kOutput, calls=%fused_computation.12 | convolution fusion | flops 7102431232 | bytes 83493904 | tf_op jit(solution)/shard_map/ikab,ikbm->iam/dot_general | solution.py:15
  1909.8 16.3 copy.98
  1926.1 77.6 %reshape.158 = bf16[13312,1,416]{2,1,0:T(2,128)(2,1)} reshape(bf16[104,128,416]{2,1,0:T(8,128)(2,1)} %copy.98) | data formatting | bytes 22151168 | tf_op jit(solution)/shard_map/convert_element_type | solution.py:16
  2003.7 87.6 %reduce.3 = bf16[13312,416]{1,0:T(8,128)(2,1)} reduce(bf16[13312,1,416]{2,1,0:T(2,128)(2,1)} %reshape.158, bf16[]{:T(256)} %broadcast.21), dimensions={1}, to_apply=%reshape.158.reduce_sub_computation | reduce | bytes 22151170 | tf_op jit(solution)/shard_map/convert_element_type | solution.py:16
  2091.3 22.4 reshape.165
  2120.1 30.4 %reshape.164 = bf16[13312,1,416]{2,1,0:T(2,128)(2,1)} reshape(bf16[8,2,346112]{2,1,0:T(2,128)(2,1)} %all-to-all-done.5) | data formatting | bytes 22151168
  2150.5 52.5 %copy.82 = bf16[13312,1,416]{0,2,1:T(8,128)(2,1)} copy(bf16[13312,1,416]{2,1,0:T(2,128)(2,1)} %reshape.164) | data formatting | bytes 22151168 | tf_op jit(solution)/shard_map/all_to_all | solution.py:46
  2218.3 19.4 copy.83
  2237.6 22.9 copy.90
  2260.5 97.7 %all-to-all-done.7 = bf16[4,2,692224]{2,1,0:T(2,128)(2,1)} async-done(((bf16[4,2,692224]{2,1,0:T(2,128)(2,1)}), bf16[4,2,692224]{2,1,0:T(2,128)(2,1)}, u32[]{:S(2)}, u32[]{:S(2)}) %all-to-all-start.7) | async-done | bytes 11075616 | tf_op jit(solution)/shard_map/all_to_all | solution.py:52
  2358.2 45.3 %reshape.166 = bf16[13312,1,416]{2,1,0:T(2,128)(2,1)} reshape(bf16[4,2,692224]{2,1,0:T(2,128)(2,1)} %all-to-all-done.7) | data formatting | bytes 22151168
  2403.5 52.7 %copy.88 = bf16[13312,1,416]{0,2,1:T(8,128)(2,1)} copy(bf16[13312,1,416]{2,1,0:T(2,128)(2,1)} %reshape.166) | data formatting | bytes 22151168 | tf_op jit(solution)/shard_map/all_to_all | solution.py:52
  2456.2 21.5 reshape.110
  2477.7 19.4 copy.89
  2497.1 40.2 %multiply_reduce_fusion.1 = (f32[]{:T(128)}, f32[]{:T(128)}, f32[1664,3328]{1,0:T(8,128)}) fusion(f32[1664,3328]{1,0:T(8,128)} %get-tuple-element.13, f32[]{:T(128)S(6)} %max.13, bf16[1664,3328]{1,0:T(8,128)(2,1)} %param.5, f32[]{:T(128)} %sqrt.10, f32[1664,3328]{1,0:T(8,128)} %get-tuple-element.15, f32[1664,3328]{1,0:T(8,128)} %copy.90, ...), kind=kLoop, calls=%fused_computation.18 | loop fusion | flops 66453504 | bytes 121831440 | tf_op jit(solution)/shard_map/reduce_sum | solution.py:60
  2537.3 42.5 %all-reduce = (f32[]{:T(128)}, f32[]{:T(128)}) all-reduce(f32[]{:T(128)} %get-tuple-element.4, f32[]{:T(128)} %get-tuple-element.3), channel_id=1, replica_groups=mesh['up'=8,'dn'=4] {'up','dn'}, use_global_device_ids=true, to_apply=%region_9.0 | all-reduce | flops 2 | bytes 16 | tf_op jit(solution)/shard_map/psum | solution.py:60
  2583.3 19.5 divide_convert_fusion
  (37 shorter events, 104.8 us)
Async XLA Ops:
  80.3 133.9 %copy-start.4 = (s32[104,5]{0,1:T(8,128)S(1)}, s32[104,5]{0,1:T(8,128)}, u32[]{:S(2)}) copy-start(s32[104,5]{0,1:T(8,128)} %param.8) | copy-start | bytes 6244
  80.3 134.0 %copy-start.5 = (s32[104,5]{0,1:T(8,128)S(1)}, s32[104,5]{0,1:T(8,128)}, u32[]{:S(2)}) copy-start(s32[104,5]{0,1:T(8,128)} %param.7) | copy-start | bytes 6244
  207.5 317.4 %all-to-all-start.2 = ((bf16[3328,4,416]{0,2,1:T(8,128)(2,1)}), bf16[3328,4,416]{0,2,1:T(8,128)(2,1)}, u32[]{:S(2)}, u32[]{:S(2)}) async-start(bf16[3328,4,416]{0,2,1:T(8,128)(2,1)} %bitcast.96), calls=%async_computation.2 | async-start | bytes 22151168 | tf_op jit(solution)/shard_map/all_to_all | solution.py:49
  214.3 399.5 %copy-start.2 = (bf16[104,5]{1,0:T(8,128)(2,1)}, bf16[104,5]{1,0:T(8,128)(2,1)S(1)}, u32[]{:S(2)}) copy-start(bf16[104,5]{1,0:T(8,128)(2,1)S(1)} %copy.61) | copy-start | bytes 3124
  214.7 372.7 %copy-start = (s32[1024]{0:T(1024)}, s32[1024]{0:T(1024)S(1)}, u32[]{:S(2)}) copy-start(s32[1024]{0:T(1024)S(1)} %pad_clamp_fusion) | copy-start | bytes 12292
  524.9 322.3 %all-to-all-start.1 = ((bf16[8,2,346112]{2,1,0:T(2,128)(2,1)}), bf16[8,2,346112]{2,1,0:T(2,128)(2,1)}, u32[]{:S(2)}, u32[]{:S(2)}) async-start(bf16[8,2,346112]{2,1,0:T(2,128)(2,1)} %reshape.159), calls=%async_computation.1 | async-start | bytes 22151168 | tf_op jit(solution)/shard_map/all_to_all | solution.py:46
  847.2 244.5 %all-to-all-start.3 = ((bf16[4,2,692224]{2,1,0:T(2,128)(2,1)}), bf16[4,2,692224]{2,1,0:T(2,128)(2,1)}, u32[]{:S(2)}, u32[]{:S(2)}) async-start(bf16[4,2,692224]{2,1,0:T(2,128)(2,1)} %reshape.161), calls=%async_computation.3 | async-start | bytes 22151168 | tf_op jit(solution)/shard_map/all_to_all | solution.py:52
  1475.6 315.9 %all-to-all-start.6 = ((bf16[3328,4,416]{0,2,1:T(8,128)(2,1)}), bf16[3328,4,416]{0,2,1:T(8,128)(2,1)}, u32[]{:S(2)}, u32[]{:S(2)}) async-start(bf16[3328,4,416]{0,2,1:T(8,128)(2,1)} %bitcast.97), calls=%async_computation.6 | async-start | bytes 22151168 | tf_op jit(solution)/shard_map/all_to_all | solution.py:49
  1500.6 31.8 %copy-start.1 = (s32[1024]{0:T(1024)S(1)}, s32[1024]{0:T(1024)}, u32[]{:S(2)}) copy-start(s32[1024]{0:T(1024)} %copy-done) | copy-start | bytes 12292
  1532.3 26.5 %copy-start.3 = (bf16[104,5]{1,0:T(8,128)(2,1)S(1)}, bf16[104,5]{1,0:T(8,128)(2,1)}, u32[]{:S(2)}) copy-start(bf16[104,5]{1,0:T(8,128)(2,1)} %copy-done.2) | copy-start | bytes 3124
  1791.5 322.3 %all-to-all-start.5 = ((bf16[8,2,346112]{2,1,0:T(2,128)(2,1)}), bf16[8,2,346112]{2,1,0:T(2,128)(2,1)}, u32[]{:S(2)}, u32[]{:S(2)}) async-start(bf16[8,2,346112]{2,1,0:T(2,128)(2,1)} %reshape.163), calls=%async_computation.5 | async-start | bytes 22151168 | tf_op jit(solution)/shard_map/all_to_all | solution.py:46
  2113.7 244.5 %all-to-all-start.7 = ((bf16[4,2,692224]{2,1,0:T(2,128)(2,1)}), bf16[4,2,692224]{2,1,0:T(2,128)(2,1)}, u32[]{:S(2)}, u32[]{:S(2)}) async-start(bf16[4,2,692224]{2,1,0:T(2,128)(2,1)} %reshape.165), calls=%async_computation.7 | async-start | bytes 22151168 | tf_op jit(solution)/shard_map/all_to_all | solution.py:52
where the time goes:
time: 2630 us; the launch traced here: 2600 us
  local copies, waits for them, and re-layouts  1360 us (52%)
  other arithmetic  469 us (18%)
  blocking collectives  381 us (14%)
  waiting for transfers between devices  194 us (7%)
  matrix products  150 us (6%)
  starting transfers between devices  39.6 us (2%)
    convert_element_type x9, local copies, waits for them, and re-layouts, hop_lead(): return result.reshape(layout).astype(jnp.bfloat16)  376 us
    convert_element_type x4, other arithmetic, hop_lead(): return result.reshape(layout).astype(jnp.bfloat16)  350 us
    unnamed x22, local copies, waits for them, and re-layouts  257 us
    all_to_all x2, blocking collectives, body(): lax.all_to_all(cube, 'up', split_axis=1, concat_axis=0, tiled=True)  254 us
    all_to_all x2, waiting for transfers between devices, body(): lax.all_to_all(hopped, 'dn', split_axis=0, concat_axis=1, tiled=True)  194 us
    another operation x8, local copies, waits for them, and re-layouts, hop_lead(): cube = matrix.reshape(layout[0] // tile_width, tile_width, -1)  122 us
    dot_general x4, matrix products, hop_lead(): jnp.einsum('ikab,ikbm->iam', signed, picked, preferred_element_type=jnp.f...  118 us
    gather x4, local copies, waits for them, and re-layouts, hop_lead(): picked = cube[tile_columns]  106 us
  transfers between devices with their start and end apart: 6, of which 2 were waited for; matrix products, arithmetic and copies ran while one was open for 59% of the time, Pallas kernels for 0%

commit v1 on v0

--- a/solution.py
+++ b/solution.py
@@ -5,6 +5,20 @@
 
 STEPS = 2
 coupling = 4.0
+
+
+def link_loads_now(page, dim_no, unit):
+    t1, v_next = (page.shape[:dim_no], page.shape[dim_no + 1 :])
+    all_values = page.reshape(*t1, unit, -1, *v_next)
+    return jnp.moveaxis(all_values, dim_no, 0)
+
+
+def _search_roads(t0, where_dim):
+    t0 = jnp.moveaxis(t0, 0, where_dim)
+    tall = t0.shape
+    return t0.reshape(
+        *tall[:where_dim], tall[where_dim] * tall[where_dim + 1], *tall[where_dim + 2 :]
+    )
 
 
 def hop_lead(matrix, signed, tile_columns):
@@ -49,7 +63,17 @@
         part = lax.all_to_all(flipped, "dn", split_axis=1, concat_axis=0, tiled=True)
         whole = part.reshape(part.shape[0], part.shape[2])
         hopped = hop_lead(whole, signed, tile_columns).reshape(part.shape)
-        returned = lax.all_to_all(hopped, "dn", split_axis=0, concat_axis=1, tiled=True)
+        m_next = lax.psum(1, axis_name="dn")
+        r2, t_next = (m_next, lax.axis_index("dn"))
+        x_new = link_loads_now(hopped, 0, r2)
+        queue = [x_new[t_next]]
+        for h in [*range(1, r2)]:
+            current_block = x_new[t_next ^ h]
+            queue.append(
+                lax.ppermute(current_block, axis_name="dn", perm=[(no, no ^ h) for no in range(r2)])
+            )
+        x_new = jnp.stack(queue)[t_next ^ jnp.arange(r2)]
+        returned = _search_roads(x_new, 1)
         hopped_down = returned.reshape(block_cols, block_rows).T
         work = (
             hopped_up.astype(jnp.float32)

time: 2630 us -> 2480 us (0.943)
  local copies, waits for them, and re-layouts: 1360 us -> 1120 us
  waiting for transfers between devices: 194 us -> 387 us
  other arithmetic: 469 us -> 375 us
    all_to_all x2, waiting for transfers between devices: 0.01 us -> 321 us  [body(): lax.all_to_all(flipped, 'dn', split_axis=1, concat_axis=0, tiled=True)]
    all_to_all x2 -> x0, waiting for transfers between devices: 194 us -> none  [body(): lax.all_to_all(hopped, 'dn', split_axis=0, concat_axis=1, tiled=True)]
    convert_element_type x4 -> x2, other arithmetic: 350 us -> 175 us  [hop_lead(): return result.reshape(layout).astype(jnp.bfloat16)]
    unnamed x22 -> x34, local copies, waits for them, and re-layouts: 257 us -> 140 us
    convert_element_type x9, local copies, waits for them, and re-layouts: 376 us -> 266 us  [hop_lead(): return result.reshape(layout).astype(jnp.bfloat16)]
    all_to_all x2 -> x0, local copies, waits for them, and re-layouts: 106 us -> none  [body(): lax.all_to_all(hopped, 'dn', split_axis=0, concat_axis=1, tiled=True)]
    convert_element_type x4 -> x0, local copies, waits for them, and re-layouts: 81.9 us -> none  [body(): hopped_down.astype(jnp.float32)]
    dynamic_slice x0 -> x2, local copies, waits for them, and re-layouts: none -> 69.4 us  [body(): queue = [x_new[t_next]]]
  transfers between devices with their start and end apart: 6 -> 10, of which waited for: 2 -> 4; matrix products, arithmetic and copies ran while one was open for 59% -> 33% of each run, Pallas kernels for 0% -> 0%
where the time goes in v1:
time: 2480 us; the launch traced here: 2460 us
  local copies, waits for them, and re-layouts  1120 us (45%)
  waiting for transfers between devices  387 us (16%)
  blocking collectives  381 us (15%)
  other arithmetic  375 us (15%)
  matrix products  150 us (6%)
  starting transfers between devices  35.7 us (1%)
    all_to_all x2, waiting for transfers between devices, body(): lax.all_to_all(flipped, 'dn', split_axis=1, concat_axis=0, tiled=True)  321 us
    convert_element_type x9, local copies, waits for them, and re-layouts, hop_lead(): return result.reshape(layout).astype(jnp.bfloat16)  266 us
    all_to_all x2, blocking collectives, body(): lax.all_to_all(cube, 'up', split_axis=1, concat_axis=0, tiled=True)  254 us
    convert_element_type x2, other arithmetic, hop_lead(): return result.reshape(layout).astype(jnp.bfloat16)  175 us
    unnamed x34, local copies, waits for them, and re-layouts  140 us
    another operation x8, local copies, waits for them, and re-layouts, hop_lead(): cube = matrix.reshape(layout[0] // tile_width, tile_width, -1)  123 us
    dot_general x4, matrix products, hop_lead(): jnp.einsum('ikab,ikbm->iam', signed, picked, preferred_element_type=jnp.f...  118 us
    gather x4, local copies, waits for them, and re-layouts, hop_lead(): picked = cube[tile_columns]  106 us
  transfers between devices with their start and end apart: 10, of which 4 were waited for; matrix products, arithmetic and copies ran while one was open for 33% of the time, Pallas kernels for 0%

profile of v1, /device:TPU:12, one launch (start us, length us, event | category | flops | bytes accessed | tf_op | source)
XLA Modules:
  0.0 2461.3 jit_solution(4745952599338156264)
XLA Ops:
  0.6 10.4 fusion
  11.1 41.6 %psum.35 = f32[]{:T(128)} all-reduce(f32[]{:T(128)} %fusion), channel_id=1, replica_groups=mesh['up'=8,'dn'=4] {'up','dn'}, use_global_device_ids=true, to_apply=%region_1.0 | all-reduce | flops 1 | bytes 8 | tf_op jit(solution)/shard_map/psum | solution.py:47
  53.3 10.6 fusion.27
  64.0 16.3 copy.74
  80.3 127.0 %all_to_all.78 = bf16[1664,8,416]{0,2,1:T(8,128)(2,1)} all-to-all(bf16[1664,8,416]{0,2,1:T(8,128)(2,1)} %bitcast.152), channel_id=1, replica_groups=mesh['up'=8,'dn'=4] {'up'}, dimensions={1} | all-to-all | bytes 22151168 | tf_op jit(solution)/shard_map/all_to_all | solution.py:57
  214.7 18.8 copy.75
  233.4 21.0 reshape_reshape.16
  254.5 10.8 copy.77
  265.3 26.4 %gather_fusion = bf16[520,128,416]{1,2,0:T(8,128)(2,1)} fusion(bf16[104,128,416]{1,2,0:T(8,128)(2,1)} %copy.77, s32[1024]{0:T(1024)S(1)} %pad_clamp_fusion.1), kind=kCustom, calls=%fused_computation | custom fusion | bytes 110757920 | tf_op jit(solution)/shard_map/gather | solution.py:28
  291.7 160.1 %all-to-all-done.2 = bf16[3328,4,416]{0,2,1:T(8,128)(2,1)} async-done(((bf16[3328,4,416]{0,2,1:T(8,128)(2,1)}), bf16[3328,4,416]{0,2,1:T(8,128)(2,1)}, u32[]{:S(2)}, u32[]{:S(2)}) %all-to-all-start.2) | async-done | bytes 11075616 | tf_op jit(solution)/shard_map/all_to_all | solution.py:63
  451.8 25.9 %copy.82 = bf16[4,3328,1,416]{1,0,3,2:T(4,128)(2,1)} copy(bf16[4,3328,1,416]{1,3,0,2:T(8,128)(2,1)} %bitcast.11) | data formatting | bytes 22151168 | tf_op jit(solution)/shard_map/all_to_all | solution.py:63
  477.7 18.8 reshape_reshape.17
  496.5 10.6 copy.83
  507.2 26.7 %gather_fusion.1 = bf16[520,128,416]{1,2,0:T(8,128)(2,1)} fusion(bf16[104,128,416]{1,2,0:T(8,128)(2,1)} %copy.83, s32[1024]{0:T(1024)S(1)} %pad_clamp_fusion.1), kind=kCustom, calls=%fused_computation.1 | custom fusion | bytes 110757920 | tf_op jit(solution)/shard_map/gather | solution.py:28
  533.8 29.4 %bitcast_convert_fusion.2 = bf16[104,128,416]{1,2,0:T(8,128)(2,1)} fusion(bf16[104,5,128,416]{2,3,1,0:T(8,128)(2,1)} %bitcast.149, bf16[104,5,128,128]{3,2,1,0:T(8,128)(2,1)} %param.6, bf16[104,5]{1,0:T(8,128)(2,1)S(1)} %copy.73), kind=kOutput, calls=%fused_computation.18 | convolution fusion | flops 7102431232 | bytes 83493904 | tf_op jit(solution)/shard_map/ikab,ikbm->iam/dot_general | solution.py:29
  563.3 19.5 copy.84
  582.8 19.4 convert_element_type.131
  602.2 34.7 %constant_dynamic-slice_fusion.7 = (bf16[1,3328,1,416]{1,0,3,2:T(2,128)(2,1)}, bf16[1,3328,1,416]{1,0,3,2:T(2,128)(2,1)}, bf16[1,3328,1,416]{1,0,3,2:T(2,128)(2,1)}, bf16[1,3328,1,416]{1,0,3,2:T(2,128)(2,1)}) fusion(bf16[4,3328,1,416]{1,0,3,2:T(4,128)(2,1)} %convert_element_type.131, s32[]{:T(128)S(6)} %select_n.40, s32[]{:T(128)S(6)} %select_n.43, ...), kind=kLoop, calls=%fused_computation.68 | loop fusion | bytes 22151184 | tf_op jit(solution)/shard_map/dynamic_slice | solution.py:69
  651.2 29.4 %bitcast_convert_fusion.3 = bf16[104,128,416]{1,2,0:T(8,128)(2,1)} fusion(bf16[104,5,128,416]{2,3,1,0:T(8,128)(2,1)} %bitcast.147, bf16[104,5,128,128]{3,2,1,0:T(8,128)(2,1)} %param.6, bf16[104,5]{1,0:T(8,128)(2,1)S(1)} %copy.73), kind=kOutput, calls=%fused_computation.19 | convolution fusion | flops 7102431232 | bytes 83493904 | tf_op jit(solution)/shard_map/ikab,ikbm->iam/dot_general | solution.py:29
  680.6 16.3 copy.111
  696.9 77.6 %reshape.199 = bf16[13312,1,416]{2,1,0:T(2,128)(2,1)} reshape(bf16[104,128,416]{2,1,0:T(8,128)(2,1)} %copy.111) | data formatting | bytes 22151168 | tf_op jit(solution)/shard_map/convert_element_type | solution.py:30
  775.0 87.5 %reduce = bf16[13312,416]{1,0:T(8,128)(2,1)} reduce(bf16[13312,1,416]{2,1,0:T(2,128)(2,1)} %reshape.199, bf16[]{:T(256)} %broadcast.62), dimensions={1}, to_apply=%reshape.199.reduce_sub_computation | reduce | bytes 22151170 | tf_op jit(solution)/shard_map/convert_element_type | solution.py:30
  862.5 21.7 reshape.201
  917.8 28.0 %pad_maximum_fusion = bf16[4,3328,1,416]{1,0,3,2:T(4,128)(2,1)S(1)} fusion(bf16[1,3328,1,416]{1,0,3,2:T(2,128)(2,1)} %copy.87, bf16[1,3328,1,416]{1,0,3,2:T(2,128)(2,1)} %copy.86, bf16[1,3328,1,416]{1,0,3,2:T(2,128)(2,1)} %copy.85, bf16[1,3328,1,416]{1,0,3,2:T(2,128)(2,1)} %get-tuple-element.23), kind=kLoop, calls=%fused_computation.26 | loop fusion | flops 44302336 | bytes 22151168 | tf_op jit(solution)/shard_map/stack | solution.py:75
  952.3 9.7 copy_bitcast_fusion.2
  974.3 37.9 %all-to-all-done.1 = bf16[8,2,346112]{2,1,0:T(2,128)(2,1)} async-done(((bf16[8,2,346112]{2,1,0:T(2,128)(2,1)}), bf16[8,2,346112]{2,1,0:T(2,128)(2,1)}, u32[]{:S(2)}, u32[]{:S(2)}) %all-to-all-start.1) | async-done | bytes 11075616 | tf_op jit(solution)/shard_map/all_to_all | solution.py:60
  1012.1 30.4 %reshape.202 = bf16[13312,1,416]{2,1,0:T(2,128)(2,1)} reshape(bf16[8,2,346112]{2,1,0:T(2,128)(2,1)} %all-to-all-done.1) | data formatting | bytes 22151168
  1042.5 52.5 %copy.80 = bf16[13312,1,416]{0,2,1:T(8,128)(2,1)} copy(bf16[13312,1,416]{2,1,0:T(2,128)(2,1)} %reshape.202) | data formatting | bytes 22151168 | tf_op jit(solution)/shard_map/all_to_all | solution.py:60
  1110.3 19.8 copy.81
  1130.0 22.8 copy.90
  1152.9 12.5 maximum_convert_fusion
  1165.4 32.2 %multiply_reduce_fusion.3 = (f32[]{:T(128)}, f32[]{:T(128)}, f32[1664,3328]{1,0:T(8,128)}, f32[1664,3328]{1,0:T(8,128)}) fusion(f32[]{:T(128)S(6)} %max.13, bf16[1664,3328]{1,0:T(8,128)(2,1)} %param.5, f32[1664,3328]{1,0:T(8,128)} %copy.90, f32[4,3328,1,416]{1,3,0,2:T(8,128)} %maximum_convert_fusion, s32[16,13312]{1,0:T(8,128)} %param.9, s32[]{:T(128)S(6)} %select_n.46, ...), kind=kOutput, calls=%fused_computation.25 | convolution fusion | flops 232667136 | bytes 99999760 | tf_op jit(solution)/shard_map/sa,sb->ab/dot_general | solution.py:43
  1197.6 42.7 %all-reduce.1 = (f32[]{:T(128)}, f32[]{:T(128)}) all-reduce(f32[]{:T(128)} %get-tuple-element.6, f32[]{:T(128)} %get-tuple-element.5), channel_id=1, replica_groups=mesh['up'=8,'dn'=4] {'up','dn'}, use_global_device_ids=true, to_apply=%region_5.0 | all-reduce | flops 2 | bytes 16 | tf_op jit(solution)/shard_map/psum | solution.py:84
  1243.5 22.7 fusion.29
  1266.2 16.3 copy.91
  1282.5 127.0 %all_to_all.79 = bf16[1664,8,416]{0,2,1:T(8,128)(2,1)} all-to-all(bf16[1664,8,416]{0,2,1:T(8,128)(2,1)} %bitcast.153), channel_id=1, replica_groups=mesh['up'=8,'dn'=4] {'up'}, dimensions={1} | all-to-all | bytes 22151168 | tf_op jit(solution)/shard_map/all_to_all | solution.py:57
  1415.8 18.8 copy.92
  1434.6 21.0 reshape_reshape.18
  1455.6 10.8 copy.93
  1466.4 26.4 %gather_fusion.2 = bf16[520,128,416]{1,2,0:T(8,128)(2,1)} fusion(bf16[104,128,416]{1,2,0:T(8,128)(2,1)} %copy.93, s32[1024]{0:T(1024)S(1)} %copy-done.1), kind=kCustom, calls=%fused_computation.2 | custom fusion | bytes 110757920 | tf_op jit(solution)/shard_map/gather | solution.py:28
  1492.9 160.9 %all-to-all-done.5 = bf16[3328,4,416]{0,2,1:T(8,128)(2,1)} async-done(((bf16[3328,4,416]{0,2,1:T(8,128)(2,1)}), bf16[3328,4,416]{0,2,1:T(8,128)(2,1)}, u32[]{:S(2)}, u32[]{:S(2)}) %all-to-all-start.5) | async-done | bytes 11075616 | tf_op jit(solution)/shard_map/all_to_all | solution.py:63
  1653.7 25.9 %copy.98 = bf16[4,3328,1,416]{1,0,3,2:T(4,128)(2,1)} copy(bf16[4,3328,1,416]{1,3,0,2:T(8,128)(2,1)} %bitcast.37) | data formatting | bytes 22151168 | tf_op jit(solution)/shard_map/all_to_all | solution.py:63
  1679.7 18.8 reshape_reshape.19
  1698.5 10.6 copy.99
  1709.1 26.7 %gather_fusion.3 = bf16[520,128,416]{1,2,0:T(8,128)(2,1)} fusion(bf16[104,128,416]{1,2,0:T(8,128)(2,1)} %copy.99, s32[1024]{0:T(1024)S(1)} %copy-done.1), kind=kCustom, calls=%fused_computation.3 | custom fusion | bytes 110757920 | tf_op jit(solution)/shard_map/gather | solution.py:28
  1735.8 29.4 %bitcast_convert_fusion = bf16[104,128,416]{1,2,0:T(8,128)(2,1)} fusion(bf16[104,5,128,416]{2,3,1,0:T(8,128)(2,1)} %bitcast.148, bf16[104,5,128,128]{3,2,1,0:T(8,128)(2,1)} %param.6, bf16[104,5]{1,0:T(8,128)(2,1)S(1)} %copy-done.3), kind=kOutput, calls=%fused_computation.16 | convolution fusion | flops 7102431232 | bytes 83493904 | tf_op jit(solution)/shard_map/ikab,ikbm->iam/dot_general | solution.py:29
  1765.2 19.5 copy.100
  1784.8 19.4 convert_element_type.146
  1804.2 34.7 %constant_dynamic-slice_fusion.2 = (bf16[1,3328,1,416]{1,0,3,2:T(2,128)(2,1)}, bf16[1,3328,1,416]{1,0,3,2:T(2,128)(2,1)}, bf16[1,3328,1,416]{1,0,3,2:T(2,128)(2,1)}, bf16[1,3328,1,416]{1,0,3,2:T(2,128)(2,1)}) fusion(bf16[4,3328,1,416]{1,0,3,2:T(4,128)(2,1)} %convert_element_type.146, s32[]{:T(128)S(6)} %select_n.40, s32[]{:T(128)S(6)} %select_n.43, ...), kind=kLoop, calls=%fused_computation.62 | loop fusion | bytes 22151184 | tf_op jit(solution)/shard_map/dynamic_slice | solution.py:69
  1852.5 29.4 %bitcast_convert_fusion.1 = bf16[104,128,416]{1,2,0:T(8,128)(2,1)} fusion(bf16[104,5,128,416]{2,3,1,0:T(8,128)(2,1)} %bitcast.146, bf16[104,5,128,128]{3,2,1,0:T(8,128)(2,1)} %param.6, bf16[104,5]{1,0:T(8,128)(2,1)S(1)} %copy-done.3), kind=kOutput, calls=%fused_computation.17 | convolution fusion | flops 7102431232 | bytes 83493904 | tf_op jit(solution)/shard_map/ikab,ikbm->iam/dot_general | solution.py:29
  1881.9 16.3 copy.112
  1898.2 77.6 %reshape.200 = bf16[13312,1,416]{2,1,0:T(2,128)(2,1)} reshape(bf16[104,128,416]{2,1,0:T(8,128)(2,1)} %copy.112) | data formatting | bytes 22151168 | tf_op jit(solution)/shard_map/convert_element_type | solution.py:30
  1975.8 87.5 %reduce.1 = bf16[13312,416]{1,0:T(8,128)(2,1)} reduce(bf16[13312,1,416]{2,1,0:T(2,128)(2,1)} %reshape.200, bf16[]{:T(256)} %broadcast.62), dimensions={1}, to_apply=%reshape.200.reduce_sub_computation | reduce | bytes 22151170 | tf_op jit(solution)/shard_map/convert_element_type | solution.py:30
  2063.3 21.7 reshape.203
  2117.4 28.0 %pad_maximum_fusion.1 = bf16[4,3328,1,416]{1,0,3,2:T(4,128)(2,1)S(1)} fusion(bf16[1,3328,1,416]{1,0,3,2:T(2,128)(2,1)} %copy.103, bf16[1,3328,1,416]{1,0,3,2:T(2,128)(2,1)} %copy.102, bf16[1,3328,1,416]{1,0,3,2:T(2,128)(2,1)} %copy.101, bf16[1,3328,1,416]{1,0,3,2:T(2,128)(2,1)} %get-tuple-element.17), kind=kLoop, calls=%fused_computation.28 | loop fusion | flops 44302336 | bytes 22151168 | tf_op jit(solution)/shard_map/stack | solution.py:75
  2172.0 12.4 maximum_convert_fusion.1
  2184.4 28.5 %all-to-all-done.4 = bf16[8,2,346112]{2,1,0:T(2,128)(2,1)} async-done(((bf16[8,2,346112]{2,1,0:T(2,128)(2,1)}), bf16[8,2,346112]{2,1,0:T(2,128)(2,1)}, u32[]{:S(2)}, u32[]{:S(2)}) %all-to-all-start.4) | async-done | bytes 11075616 | tf_op jit(solution)/shard_map/all_to_all | solution.py:60
  2213.0 30.4 %reshape.204 = bf16[13312,1,416]{2,1,0:T(2,128)(2,1)} reshape(bf16[8,2,346112]{2,1,0:T(2,128)(2,1)} %all-to-all-done.4) | data formatting | bytes 22151168
  2243.4 52.5 %copy.96 = bf16[13312,1,416]{0,2,1:T(8,128)(2,1)} copy(bf16[13312,1,416]{2,1,0:T(2,128)(2,1)} %reshape.204) | data formatting | bytes 22151168 | tf_op jit(solution)/shard_map/all_to_all | solution.py:60
  2311.3 19.4 copy.97
  2330.7 22.8 copy.106
  2353.5 40.2 %multiply_reduce_fusion.1 = (f32[]{:T(128)}, f32[]{:T(128)}, f32[1664,3328]{1,0:T(8,128)}) fusion(f32[1664,3328]{1,0:T(8,128)} %get-tuple-element.13, f32[]{:T(128)S(6)} %max.13, bf16[1664,3328]{1,0:T(8,128)(2,1)} %param.5, f32[]{:T(128)} %sqrt.10, f32[1664,3328]{1,0:T(8,128)} %get-tuple-element.27, f32[1664,3328]{1,0:T(8,128)} %copy.106, ...), kind=kLoop, calls=%fused_computation.22 | loop fusion | flops 66453504 | bytes 121831440 | tf_op jit(solution)/shard_map/reduce_sum | solution.py:84
  2393.8 42.6 %all-reduce = (f32[]{:T(128)}, f32[]{:T(128)}) all-reduce(f32[]{:T(128)} %get-tuple-element.4, f32[]{:T(128)} %get-tuple-element.3), channel_id=1, replica_groups=mesh['up'=8,'dn'=4] {'up','dn'}, use_global_device_ids=true, to_apply=%region_9.0 | all-reduce | flops 2 | bytes 16 | tf_op jit(solution)/shard_map/psum | solution.py:84
  2439.3 19.4 divide_convert_fusion
  (75 shorter events, 184.9 us)
Async XLA Ops:
  207.3 6.9 copy-start.6
  207.3 7.2 copy-start.5
  207.3 244.4 %all-to-all-start.2 = ((bf16[3328,4,416]{0,2,1:T(8,128)(2,1)}), bf16[3328,4,416]{0,2,1:T(8,128)(2,1)}, u32[]{:S(2)}, u32[]{:S(2)}) async-start(bf16[3328,4,416]{0,2,1:T(8,128)(2,1)} %bitcast.138), calls=%async_computation.2 | async-start | bytes 22151168 | tf_op jit(solution)/shard_map/all_to_all | solution.py:63
  214.6 436.5 %copy-start.2 = (bf16[104,5]{1,0:T(8,128)(2,1)}, bf16[104,5]{1,0:T(8,128)(2,1)S(1)}, u32[]{:S(2)}) copy-start(bf16[104,5]{1,0:T(8,128)(2,1)S(1)} %copy.73) | copy-start | bytes 3124
  214.7 292.5 %copy-start = (s32[1024]{0:T(1024)}, s32[1024]{0:T(1024)S(1)}, u32[]{:S(2)}) copy-start(s32[1024]{0:T(1024)S(1)} %pad_clamp_fusion.1) | copy-start | bytes 12292
  636.9 11.0 slice-start.2
  639.9 7.9 slice-start.3
  639.9 252.2 %collective-permute-start = (bf16[3328,1,416]{0,2,1:T(8,128)(2,1)S(1)}, bf16[3328,1,416]{0,2,1:T(8,128)(2,1)}, u32[]{:S(2)}, u32[]{:S(2)}) collective-permute-start(bf16[3328,1,416]{0,2,1:T(8,128)(2,1)S(1)} %bitcast.164), channel_id=1, source_target_pairs={{0,1},{1,0},{2,3},{3,2},{4,5},{5,4},{6,7},{7,6},{8,9},{9,8},{10,11... | collective-permute-start | bytes 8306696 | tf_op jit(solution)/shard_map/ppermute | solution.py:73
  647.8 252.9 %collective-permute-start.1 = (bf16[3328,1,416]{0,2,1:T(8,128)(2,1)}, bf16[3328,1,416]{0,2,1:T(8,128)(2,1)}, u32[]{:S(2)}, u32[]{:S(2)}) collective-permute-start(bf16[3328,1,416]{0,2,1:T(8,128)(2,1)} %bitcast.136), channel_id=1, source_target_pairs={{0,2},{1,3},{2,0},{3,1},{4,6},{5,7},{6,4},{7,5},{8,10},{9,11},{10,... | collective-permute-start | bytes 8306696 | tf_op jit(solution)/shard_map/ppermute | solution.py:73
  649.7 259.4 %collective-permute-start.2 = (bf16[3328,1,416]{0,2,1:T(8,128)(2,1)}, bf16[3328,1,416]{0,2,1:T(8,128)(2,1)}, u32[]{:S(2)}, u32[]{:S(2)}) collective-permute-start(bf16[3328,1,416]{0,2,1:T(8,128)(2,1)} %bitcast.135), channel_id=1, source_target_pairs={{0,3},{1,2},{2,1},{3,0},{4,7},{5,6},{6,5},{7,4},{8,11},{9,10},{10,... | collective-permute-start | bytes 8306696 | tf_op jit(solution)/shard_map/ppermute | solution.py:73
  884.2 127.9 %all-to-all-start.1 = ((bf16[8,2,346112]{2,1,0:T(2,128)(2,1)}), bf16[8,2,346112]{2,1,0:T(2,128)(2,1)}, u32[]{:S(2)}, u32[]{:S(2)}) async-start(bf16[8,2,346112]{2,1,0:T(2,128)(2,1)} %reshape.201), calls=%async_computation.1 | async-start | bytes 22151168 | tf_op jit(solution)/shard_map/all_to_all | solution.py:60
  892.2 75.9 %copy-start.4 = (s32[1024]{0:T(1024)}, s32[1024]{0:T(1024)S(1)}, u32[]{:S(2)}) copy-start(s32[1024]{0:T(1024)S(1)} %pad_clamp_fusion) | copy-start | bytes 12292
  1409.6 244.2 %all-to-all-start.5 = ((bf16[3328,4,416]{0,2,1:T(8,128)(2,1)}), bf16[3328,4,416]{0,2,1:T(8,128)(2,1)}, u32[]{:S(2)}, u32[]{:S(2)}) async-start(bf16[3328,4,416]{0,2,1:T(8,128)(2,1)} %bitcast.139), calls=%async_computation.5 | async-start | bytes 22151168 | tf_op jit(solution)/shard_map/all_to_all | solution.py:63
  1455.6 10.8 copy-start.1
  1709.1 26.7 %copy-start.3 = (bf16[104,5]{1,0:T(8,128)(2,1)S(1)}, bf16[104,5]{1,0:T(8,128)(2,1)}, u32[]{:S(2)}) copy-start(bf16[104,5]{1,0:T(8,128)(2,1)} %copy-done.2) | copy-start | bytes 3124
  1838.9 11.0 slice-start
  1842.0 8.0 slice-start.1
  1842.0 249.7 %collective-permute-start.3 = (bf16[3328,1,416]{0,2,1:T(8,128)(2,1)S(1)}, bf16[3328,1,416]{0,2,1:T(8,128)(2,1)}, u32[]{:S(2)}, u32[]{:S(2)}) collective-permute-start(bf16[3328,1,416]{0,2,1:T(8,128)(2,1)S(1)} %bitcast.165), channel_id=1, source_target_pairs={{0,1},{1,0},{2,3},{3,2},{4,5},{5,4},{6,7},{7,6},{8,9},{9,8},{10,11... | collective-permute-start | bytes 8306696 | tf_op jit(solution)/shard_map/ppermute | solution.py:73
  1849.1 251.1 %collective-permute-start.4 = (bf16[3328,1,416]{0,2,1:T(8,128)(2,1)}, bf16[3328,1,416]{0,2,1:T(8,128)(2,1)}, u32[]{:S(2)}, u32[]{:S(2)}) collective-permute-start(bf16[3328,1,416]{0,2,1:T(8,128)(2,1)} %bitcast.133), channel_id=1, source_target_pairs={{0,2},{1,3},{2,0},{3,1},{4,6},{5,7},{6,4},{7,5},{8,10},{9,11},{10,... | collective-permute-start | bytes 8306696 | tf_op jit(solution)/shard_map/ppermute | solution.py:73
  1851.8 256.8 %collective-permute-start.5 = (bf16[3328,1,416]{0,2,1:T(8,128)(2,1)}, bf16[3328,1,416]{0,2,1:T(8,128)(2,1)}, u32[]{:S(2)}, u32[]{:S(2)}) collective-permute-start(bf16[3328,1,416]{0,2,1:T(8,128)(2,1)} %bitcast.132), channel_id=1, source_target_pairs={{0,3},{1,2},{2,1},{3,0},{4,7},{5,6},{6,5},{7,4},{8,11},{9,10},{10,... | collective-permute-start | bytes 8306696 | tf_op jit(solution)/shard_map/ppermute | solution.py:73
  2085.0 128.0 %all-to-all-start.4 = ((bf16[8,2,346112]{2,1,0:T(2,128)(2,1)}), bf16[8,2,346112]{2,1,0:T(2,128)(2,1)}, u32[]{:S(2)}, u32[]{:S(2)}) async-start(bf16[8,2,346112]{2,1,0:T(2,128)(2,1)} %reshape.203), calls=%async_computation.4 | async-start | bytes 22151168 | tf_op jit(solution)/shard_map/all_to_all | solution.py:60
